TPU v7x, 32 devices: a whole 2x2x4 slice. The times are simulated.
32 devices in a mesh: cfg: 2 (over y), seq: 8 (over z, core), tp: 2 (over x).
Axes of the slice: x: 2, y: 2, z: 4, core: 2. Of those that a mesh axis runs over, the one named last changes fastest.
Arguments:
- queries: bfloat16 [2, 3840, 5120], P('cfg', 'seq', 'tp'), may hold values from -5 to 5
- keys: bfloat16 [2, 3840, 5120], P('cfg', 'seq', 'tp'), may hold values from -5 to 5
- values: bfloat16 [2, 3840, 5120], P('cfg', 'seq', 'tp'), may hold values from -5 to 5
- text_keys: bfloat16 [2, 512, 5120], P('cfg', None, 'tp'), may hold values from -7.5 to 7.5
- text_values: bfloat16 [2, 512, 5120], P('cfg', None, 'tp'), may hold values from -5 to 5
- prompt_lengths: int32 [2], P('cfg'), may hold values from 64 to 512
- frame_counts: int32 [8], P('seq'), may hold values from 240 to 480
- out_weight: bfloat16 [5120, 5120], P('tp'), may hold values from -0.5 to 0.5
Outputs:
- velocity: bfloat16 [3840, 5120], P('seq', ('tp', 'cfg'))
All inputs are finite; a program needn't handle non-finite values.
Results may differ from a plain program's by a relative error of at most 0.015.
Values may be sent and summed in bfloat16 or wider, within the bound.
A program may use at most 320 MiB of HBM per device.

v0:
```python
import jax
import jax.numpy as jnp
from jax import lax
from jax.sharding import PartitionSpec as P

HEAD_DIM = 128
FRAME_SLOTS = 480


GUIDANCE = 5.0
RESCALE = 0.7
NEGATIVE = -1e30


def frame_valid(positions, counts_table):
    frame_index = positions // FRAME_SLOTS
    slot_index = positions % FRAME_SLOTS
    frame_ids = jnp.arange(counts_table.shape[0], dtype=jnp.int32)
    frame_limit = jnp.sum(
        jnp.where(frame_index[:, None] == frame_ids[None, :], counts_table[None, :], 0), axis=1
    )
    return slot_index < frame_limit


def attend_block(carry, key_rows, value_rows, query_heads, key_mask):
    row_max, weight_sum, mixed_sum = carry
    head_count = query_heads.shape[1]
    key_heads = key_rows.reshape(key_rows.shape[0], head_count, HEAD_DIM)
    value_heads = value_rows.reshape(value_rows.shape[0], head_count, HEAD_DIM)
    scores = jnp.einsum(
        "qhd,khd->hqk", query_heads, key_heads, preferred_element_type=jnp.float32
    ) * HEAD_DIM ** (-0.5)
    scores = jnp.where(key_mask[None, None, :], scores, NEGATIVE)
    new_max = jnp.maximum(row_max, jnp.max(scores, axis=2))
    shrink = jnp.exp(row_max - new_max)
    weights = jnp.exp(scores - new_max[:, :, None])
    weight_sum = weight_sum * shrink + jnp.sum(weights, axis=2)
    mixed_sum = mixed_sum * shrink[:, :, None] + jnp.einsum(
        "hqk,khd->hqd",
        weights.astype(jnp.bfloat16),
        value_heads,
        preferred_element_type=jnp.float32,
    )
    return (new_max, weight_sum, mixed_sum)


def body(queries, keys, values, text_keys, text_values, prompt_lengths, frame_counts, out_weight):
    row_count = queries.shape[1]
    head_cols = queries.shape[2]
    head_count = head_cols // HEAD_DIM
    all_counts = lax.all_gather(frame_counts, "seq", axis=0, tiled=True)
    query_heads = queries[0].reshape(row_count, head_count, HEAD_DIM)
    text_mask = jnp.arange(text_keys.shape[1], dtype=jnp.int32) < prompt_lengths[0]
    empty_state = (
        jnp.full((head_count, row_count), NEGATIVE, jnp.float32),
        jnp.zeros((head_count, row_count), jnp.float32),
        jnp.zeros((head_count, row_count, HEAD_DIM), jnp.float32),
    )
    text_state = attend_block(empty_state, text_keys[0], text_values[0], query_heads, text_mask)
    key_rows = lax.all_gather(keys[0], "seq", axis=0, tiled=True)
    value_rows = lax.all_gather(values[0], "seq", axis=0, tiled=True)
    positions = jnp.arange(key_rows.shape[0], dtype=jnp.int32)
    row_max, weight_sum, mixed_sum = attend_block(
        text_state, key_rows, value_rows, query_heads, frame_valid(positions, all_counts)
    )
    attended = (
        jnp.transpose(mixed_sum / weight_sum[:, :, None], (1, 0, 2))
        .reshape(row_count, head_cols)
        .astype(jnp.bfloat16)
    )
    projected = (
        lax.psum_scatter(
            lax.dot_general(
                out_weight, attended, (((0,), (1,)), ((), ())), preferred_element_type=jnp.float32
            ).astype(jnp.bfloat16),
            "tp",
            scatter_dimension=0,
            tiled=True,
        )
        .astype(jnp.float32)
        .T
    )
    branch = projected.astype(jnp.bfloat16)[None]
    half_cols = head_cols // 2
    gathered = lax.all_gather(branch, "cfg", axis=0, tiled=True)
    paired = lax.dynamic_slice_in_dim(gathered, lax.axis_index("cfg") * half_cols, half_cols, 2)
    conditional = paired[0].astype(jnp.float32)
    unconditional = paired[1].astype(jnp.float32)
    guided = unconditional + GUIDANCE * (conditional - unconditional)
    token_weights = frame_valid(jnp.arange(row_count, dtype=jnp.int32), frame_counts).astype(
        jnp.float32
    )

    def local_sum(field_rows):
        return jnp.dot(token_weights, field_rows, precision=lax.Precision.HIGHEST)

    guided_sum, guided_square, cond_sum, cond_square = lax.psum(
        (
            local_sum(guided),
            local_sum(guided * guided),
            local_sum(conditional),
            local_sum(conditional * conditional),
        ),
        "seq",
    )
    valid_total = jnp.sum(all_counts).astype(jnp.float32)
    guided_mean = guided_sum / valid_total
    guided_var = guided_square / valid_total - guided_mean * guided_mean
    cond_mean = cond_sum / valid_total
    cond_var = cond_square / valid_total - cond_mean * cond_mean
    std_ratio = jnp.sqrt((cond_var + 1.0) / (guided_var + 1.0))
    factor = RESCALE * std_ratio + (1.0 - RESCALE)
    return (guided_mean + (guided - guided_mean) * factor).astype(jnp.bfloat16)


def solution(mesh):
    placed = (
        P("cfg", "seq", "tp"),
        P("cfg", "seq", "tp"),
        P("cfg", "seq", "tp"),
        P("cfg", None, "tp"),
        P("cfg", None, "tp"),
        P("cfg"),
        P("seq"),
        P("tp", None),
    )
    return jax.shard_map(
        body, mesh=mesh, in_specs=placed, out_specs=P("seq", ("tp", "cfg")), check_vma=False
    )
```

profile of v0, /device:TPU:0, one launch (start us, length us, event | category | flops | bytes accessed | tf_op | source)
XLA Modules:
  0.0 636.8 jit_solution(17651519796824386608)
XLA Ops:
  10.0 10.6 %all-reduce = s32[8]{0:T(128)S(1)} all-reduce(s32[8]{0:T(128)S(1)} %dynamic-update-slice), channel_id=1, replica_groups=mesh['cfg'=2,'seq'=8,'tp'=2] {'seq'}, use_global_device_ids=true, to_apply=%add | all-reduce | flops 8 | bytes 64
  20.6 3.2 copy.37
  24.4 4.5 copy.38
  28.9 4.4 copy.41
  33.5 12.2 %fusion.6 = (f32[20,480]{1,0:T(8,128)S(1)}, f32[20,480,512]{2,1,0:T(8,128)}) fusion(pred[512]{0:T(512)(128)(4,1)S(1)} %iota_compare_fusion.2, bf16[480,20,128]{0,2,1:T(8,128)(2,1)S(1)} %bitcast.86, bf16[512,20,128]{0,2,1:T(8,128)(2,1)} %bitcast.89), kind=kOutput, calls=%fused_computation.9 | convolution fusion | flops 1273027200 | bytes 24778752 | tf_op jit(solution)/shard_map/qhd,khd->hqk/dot_general | solution.py:30
  45.7 140.8 %all-gather.7.cloned.1.call-done = bf16[1,3840,2560]{2,1,0:T(8,128)(2,1)} async-done(((bf16[1,480,2560]{2,1,0:T(8,128)(2,1)}), bf16[1,3840,2560]{2,1,0:T(8,128)(2,1)}) %all-gather.7.cloned.1.call-update) | async-done | bytes 19660816 | tf_op jit(solution)/shard_map/all_gather | solution.py:60
  186.5 25.5 %copy.43 = bf16[1,3840,2560]{1,2,0:T(8,128)(2,1)} copy(bf16[1,3840,2560]{2,1,0:T(8,128)(2,1)} %all-gather.7.cloned.1.call-done) | data formatting | bytes 39321600 | tf_op jit(solution)/shard_map/all_gather | solution.py:60
  211.9 58.6 %fusion = (f32[20,480]{1,0:T(8,128)S(1)}, f32[20,480,3840]{2,1,0:T(8,128)}) fusion(pred[3840]{0:T(1024)(128)(4,1)S(1)} %fusion.37, bf16[480,20,128]{0,2,1:T(8,128)(2,1)S(1)} %bitcast.87, bf16[3840,20,128]{0,2,1:T(8,128)(2,1)} %bitcast.85), kind=kOutput, calls=%fused_computation.2 | convolution fusion | flops 9547766784 | bytes 169616640 | tf_op jit(solution)/shard_map/qhd,khd->hqk/dot_general | solution.py:30
  270.5 9.7 %fusion.7 = f32[20,480]{1,0:T(8,128)S(1)} fusion(f32[20,480,512]{2,1,0:T(8,128)} %get-tuple-element.19, f32[20,480]{1,0:T(8,128)S(1)} %get-tuple-element.13, pred[512]{0:T(512)(128)(4,1)S(1)} %iota_compare_fusion.2), kind=kLoop, calls=%fused_computation.10 | loop fusion | flops 19651200 | bytes 19738112 | tf_op jit(solution)/shard_map/reduce_sum | solution.py:37
  280.2 45.5 %fusion.1 = f32[20,480]{1,0:T(8,128)S(1)} fusion(f32[20,480,3840]{2,1,0:T(8,128)} %get-tuple-element.17, f32[20,480]{1,0:T(8,128)S(1)} %get-tuple-element.12, pred[3840]{0:T(1024)(128)(4,1)S(1)} %fusion.37), kind=kLoop, calls=%fused_computation.3 | loop fusion | flops 147446400 | bytes 147536640 | tf_op jit(solution)/shard_map/reduce_sum | solution.py:37
  325.8 10.5 %fusion.9 = f32[20,480,128]{2,1,0:T(8,128)} fusion(bf16[512,20,128]{0,2,1:T(8,128)(2,1)S(1)} %bitcast.95, f32[20,480,512]{2,1,0:T(8,128)} %get-tuple-element.19, f32[20,480]{1,0:T(8,128)S(1)} %get-tuple-element.13, pred[512]{0:T(512)(128)(4,1)S(1)} %iota_compare_fusion.2), kind=kOutput, calls=%fused_computation.12 | convolution fusion | flops 1277952000 | bytes 27236352 | tf_op jit(solution)/shard_map/hqk,khd->hqd/dot_general | solution.py:38
  336.2 24.8 %all-gather.9.cloned.1.call-done = bf16[1,3840,2560]{2,1,0:T(8,128)(2,1)} async-done(((bf16[1,480,2560]{2,1,0:T(8,128)(2,1)}), bf16[1,3840,2560]{2,1,0:T(8,128)(2,1)}) %all-gather.9.cloned.1.call-update) | async-done | bytes 19660816 | tf_op jit(solution)/shard_map/all_gather | solution.py:61
  361.0 24.1 %copy.46 = bf16[1,3840,2560]{1,2,0:T(8,128)(2,1)} copy(bf16[1,3840,2560]{2,1,0:T(8,128)(2,1)} %all-gather.9.cloned.1.call-done) | data formatting | bytes 39321600 | tf_op jit(solution)/shard_map/all_gather | solution.py:61
  385.1 55.6 %fusion.17 = bf16[480,20,128]{2,0,1:T(8,128)(2,1)} fusion(f32[20,480,128]{2,1,0:T(8,128)} %fusion.9, f32[480,20]{0,1:T(8,128)S(1)} %get-tuple-element.9, f32[480,20]{0,1:T(8,128)S(1)} %get-tuple-element.10, f32[480,20]{0,1:T(8,128)S(1)} %get-tuple-element.11, bf16[3840,20,128]{0,2,1:T(8,128)(2,1)} %bitcast.88, f32[20,480,3840]{2,1,0:T(8,128)} %get-tuple-element.17, ...), kind=kOutput, calls=%fused_computation.21 | convolution fusion | flops 9590784000 | bytes 174647040 | tf_op jit(solution)/shard_map/hqk,khd->hqd/dot_general | solution.py:38
  440.7 2.9 copy.48
  443.6 19.5 %fusion.15 = bf16[5120,480]{0,1:T(8,128)(2,1)} fusion(bf16[480,2560]{0,1:T(8,128)(2,1)S(1)} %bitcast.96, bf16[2560,5120]{1,0:T(8,128)(2,1)} %param.15), kind=kOutput, calls=%fused_computation.18 | convolution fusion | flops 12585369600 | bytes 33587200 | tf_op jit(solution)/shard_map/dot_general | solution.py:73
  463.2 60.5 %reduce-scatter.2.cloned.1.call-done = bf16[2560,480]{0,1:T(8,128)(2,1)} async-done(((bf16[5120,480]{0,1:T(8,128)(2,1)}), bf16[2560,480]{0,1:T(8,128)(2,1)}) %reduce-scatter.2.cloned.1.call-update) | async-done | bytes 2457616 | tf_op jit(solution)/shard_map/reduce_scatter | solution.py:72
  525.1 65.0 %all-gather.11.cloned.1.call-done = bf16[960,2560]{1,0:T(8,128)(2,1)} async-done(((bf16[480,2560]{1,0:T(8,128)(2,1)}), bf16[960,2560]{1,0:T(8,128)(2,1)}) %all-gather.11.cloned.1.call-update) | async-done | bytes 4915216 | tf_op jit(solution)/shard_map/all_gather | solution.py:85
  590.0 1.7 convolution_reduce_fusion
  591.7 2.4 fusion.28
  594.2 2.9 fusion.29
  597.2 1.4 fusion.30
  598.5 28.4 %all-reduce.1 = (f32[1280]{0:T(1024)S(1)}, f32[1280]{0:T(1024)S(1)}, f32[1280]{0:T(1024)S(1)}, f32[1280]{0:T(1024)S(1)}) all-reduce(f32[1280]{0:T(1024)S(1)} %fusion.30, f32[1280]{0:T(1024)S(1)} %convolution_reduce_fusion, f32[1280]{0:T(1024)S(1)} %fusion.28, f32[1280]{0:T(1024)S(1)} %fusion.29), channel_id=1, replica_groups=mesh['cfg'=2,'seq'=8,'tp'=2] {'seq'}, use_global_device_ids=true, to_apply=%region_10.11 | all-reduce | flops 5120 | bytes 40960 | tf_op jit(solution)/shard_map/psum | solution.py:97
  626.9 3.4 add_convert_fusion
  (31 shorter events, 3.7 us)
Async XLA Ops:
  6.5 2.2 copy-start.4
  6.5 179.9 %all-gather.7.cloned.1.call-start = ((), (), s32[]{:S(2)}) async-start(), calls=%async_computation.2 | async-start | bytes 22118400 | tf_op jit(solution)/shard_map/all_gather | solution.py:60
  7.3 353.8 %all-gather.9.cloned.1.call-start = ((), (), s32[]{:S(2)}) async-start(), calls=%async_computation.3 | async-start | bytes 22118400 | tf_op jit(solution)/shard_map/all_gather | solution.py:61
  8.0 515.7 %reduce-scatter.2.cloned.1.call-start = ((), (), s32[]{:S(2)}) async-start(), calls=%async_computation.1 | async-start | bytes 7372800 | tf_op jit(solution)/shard_map/reduce_scatter | solution.py:72
  20.6 12.8 %copy-start.2 = (s32[8]{0:T(128)}, s32[8]{0:T(128)S(1)}, u32[]{:S(2)}) copy-start(s32[8]{0:T(128)S(1)} %all-reduce) | copy-start | bytes 100
  280.2 45.6 %copy-start.1 = (bf16[1,512,2560]{1,2,0:T(8,128)(2,1)S(1)}, bf16[1,512,2560]{1,2,0:T(8,128)(2,1)}, u32[]{:S(2)}) copy-start(bf16[1,512,2560]{1,2,0:T(8,128)(2,1)} %copy.41) | copy-start | bytes 7864324
  463.2 60.6 %copy-start.3 = (s32[8]{0:T(128)S(1)}, s32[8]{0:T(128)}, u32[]{:S(2)}) copy-start(s32[8]{0:T(128)} %copy-done.2) | copy-start | bytes 100
  463.2 126.8 %all-gather.11.cloned.1.call-start = ((), (), s32[]{:S(2)}) async-start(), calls=%async_computation.4 | async-start | bytes 7372800 | tf_op jit(solution)/shard_map/all_gather | solution.py:85
  590.0 7.1 %copy-start = (bf16[960,2560]{1,0:T(8,128)(2,1)S(1)}, bf16[960,2560]{1,0:T(8,128)(2,1)}, u32[]{:S(2)}) copy-start(bf16[960,2560]{1,0:T(8,128)(2,1)} %all-gather.11.cloned.1.call-done) | copy-start | bytes 14745604
Sparse Core Ops, SparseCore 0:
  9.0 177.4 all-gather.6
  188.1 172.8 all-gather.8
  463.3 60.3 reduce-scatter.1
  525.1 64.8 all-gather.10
where the time goes:
time: 639 us; the launch traced here: 637 us
  waiting for transfers between devices  292 us (46%)
  matrix products  165 us (26%)
  local copies, waits for them, and re-layouts  65.8 us (10%)
  other arithmetic  59.5 us (9%)
  blocking collectives  39 us (6%)
  between operations  15.2 us (2%)
    all_gather x1, waiting for transfers between devices, body(): key_rows = lax.all_gather(keys[0], 'seq', axis=0, tiled=True)  141 us
    dot_general x2, matrix products, attend_block(): jnp.einsum('qhd,khd->hqk', query_heads, key_heads, preferred_element_type...  70.7 us
    dot_general x2, matrix products, attend_block(): jnp.einsum('hqk,khd->hqd', weights.astype(jnp.bfloat16), value_heads, pre...  66.1 us
    all_gather x1, waiting for transfers between devices, body(): gathered = lax.all_gather(branch, 'cfg', axis=0, tiled=True)  65 us
    reduce_scatter x1, waiting for transfers between devices, body(): lax.psum_scatter(lax.dot_general(out_weight, attended, (((0,), (1,)), (()...  60.5 us
    reduce_sum x2, other arithmetic, attend_block(): weight_sum = weight_sum * shrink + jnp.sum(weights, axis=2)  55.2 us
    psum x1, blocking collectives, body(): lax.psum((local_sum(guided), local_sum(guided * guided), local_sum(condit...  28.4 us
    all_gather x1, local copies, waits for them, and re-layouts, body(): key_rows = lax.all_gather(keys[0], 'seq', axis=0, tiled=True)  25.5 us
  transfers between devices with their start and end apart: 4, of which 4 were waited for; matrix products, arithmetic and copies ran while one was open for 28% of the time, Pallas kernels for 0%

commit v1 on v0

v1 whole, which is shorter than its diff:
```python
import functools

import jax
import jax.numpy as jnp
from jax import lax
from jax.experimental import pallas as pl
from jax.experimental.pallas import tpu as pltpu
from jax.sharding import PartitionSpec as P

HEAD_DIM = 128
GUIDANCE = 5.0
RESCALE = 0.7
NEGATIVE = -1e30
LOG2E = 1.4426950408889634
CORES = 2
MESH = pl.DeviceIdType.MESH


def chunk_rows(total, limit):
    for unit in (256, 128, 16):
        for size in range(limit // unit * unit, 0, -unit):
            if total % size == 0:
                return size
    return total


def attention_kernel(
    n, chips, group, rows, text,
    q, k, v, tk, tv, counts, lengths,
    out,
    qb, kb, vb, tkb, tvb, cb, bias, tbias, ob,
    send, recv, fsend, frecv, csend, crecv, local, tlocal, osend, orecv,
):
    me = lax.axis_index("seq")
    core = lax.rem(me, CORES)
    chip = lax.div(me, CORES)
    partner = chip * CORES + (CORES - 1 - core)
    scale = LOG2E * HEAD_DIM ** (-0.5)

    def cols(owner, head):
        return pl.ds(pl.multiple_of((owner * group + head) * HEAD_DIM, HEAD_DIM), HEAD_DIM)

    def slot(index):
        return pl.ds(pl.multiple_of(index * rows, 16), rows)

    def chip_at(step):
        return lax.rem(chip + step, chips)

    def chip_back(step):
        return lax.rem(chip + chips - step, chips)

    barrier = pltpu.get_barrier_semaphore()
    for step in range(1, n):
        pl.semaphore_signal(
            barrier, inc=1, device_id={"seq": lax.rem(me + step, n)}, device_id_type=MESH
        )
    pl.semaphore_wait(barrier, n - 1)

    def count_copy(step):
        return pltpu.make_async_remote_copy(
            src_ref=counts, dst_ref=cb.at[me], send_sem=csend.at[step - 1],
            recv_sem=crecv.at[step - 1],
            device_id={"seq": lax.rem(me + step, n)}, device_id_type=MESH,
        )

    def block_copies(head, step):
        target = chip_at(step)
        device = {"seq": target * CORES + core}
        made = []
        for index, (src, dst) in enumerate(
            ((k, kb.at[head, slot(me)]), (v, vb.at[head, slot(me)]), (q, qb.at[head, chip]))
        ):
            made.append(pltpu.make_async_remote_copy(
                src_ref=src.at[:, cols(target, head)], dst_ref=dst,
                send_sem=send.at[index, head, step - 1],
                recv_sem=recv.at[index, head, step - 1],
                device_id=device, device_id_type=MESH,
            ))
        return made

    def own_copies(head):
        return [
            pltpu.make_async_copy(k.at[:, cols(chip, head)], kb.at[head, slot(me)], local.at[0, head]),
            pltpu.make_async_copy(v.at[:, cols(chip, head)], vb.at[head, slot(me)], local.at[1, head]),
            pltpu.make_async_copy(q.at[:, cols(chip, head)], qb.at[head, chip], local.at[2, head]),
            pltpu.make_async_copy(tk.at[:, cols(chip, head)], tkb.at[head], tlocal.at[0, head]),
            pltpu.make_async_copy(tv.at[:, cols(chip, head)], tvb.at[head], tlocal.at[1, head]),
        ]

    def own_forward(head):
        return [
            pltpu.make_async_remote_copy(
                src_ref=src.at[:, cols(chip, head)], dst_ref=dst.at[head, slot(me)],
                send_sem=fsend.at[index, head, 0], recv_sem=frecv.at[index, head, 0],
                device_id={"seq": partner}, device_id_type=MESH,
            )
            for index, (src, dst) in enumerate(((k, kb), (v, vb)))
        ]

    def forward(index, head, step):
        buf = (kb, vb)[index]
        where = slot(chip_back(step) * CORES + core)
        return pltpu.make_async_remote_copy(
            src_ref=buf.at[head, where], dst_ref=buf.at[head, where],
            send_sem=fsend.at[index, head, step], recv_sem=frecv.at[index, head, step],
            device_id={"seq": partner}, device_id_type=MESH,
        )

    def out_copy(head, step):
        target = chip_at(step)
        return pltpu.make_async_remote_copy(
            src_ref=ob.at[head, target], dst_ref=out.at[:, cols(chip, head)],
            send_sem=osend.at[head, step], recv_sem=orecv.at[head, step],
            device_id={"seq": target * CORES + core}, device_id_type=MESH,
        )

    def own_out(head):
        return pltpu.make_async_copy(
            ob.at[head, chip], out.at[:, cols(chip, head)], osend.at[head, 0]
        )

    for step in range(1, n):
        count_copy(step).start()

    def start_head(head, _):
        for step in range(1, chips):
            for copy in block_copies(head, step):
                copy.start()
        for copy in own_copies(head):
            copy.start()
        for copy in own_forward(head):
            copy.start()
        return 0

    lax.fori_loop(0, group, start_head, 0)

    cb[me] = counts[...]
    for step in range(1, n):
        count_copy(step).wait()
    lane = lax.broadcasted_iota(jnp.int32, (rows, HEAD_DIM), 1)
    place = lax.broadcasted_iota(jnp.int32, (rows, HEAD_DIM), 0)
    for source in range(n):
        limit = cb[source][0:1, :]
        bias[source * rows:(source + 1) * rows, :] = jnp.where(
            (lane == 0) & (place >= limit), NEGATIVE, 0.0
        ).astype(jnp.bfloat16)
    tlane = lax.broadcasted_iota(jnp.int32, (text, HEAD_DIM), 1)
    tplace = lax.broadcasted_iota(jnp.int32, (text, HEAD_DIM), 0)
    tbias[...] = jnp.where(
        (tlane == 0) & (tplace >= lengths[0:1, :]), NEGATIVE, 0.0
    ).astype(jnp.bfloat16)

    total = n * rows
    size = chunk_rows(total, 768)

    def ones(length):
        return jnp.where(
            lax.broadcasted_iota(jnp.int32, (length, HEAD_DIM), 1) == 0, 1.0, 0.0
        ).astype(jnp.bfloat16)

    def one_head(head, _):
        for copy in own_copies(head):
            copy.wait()
        for step in range(1, chips):
            made = block_copies(head, step)
            for index in range(2):
                made[index].wait()
                forward(index, head, step).start()
            made[2].wait()
        for copy in own_forward(head):
            copy.wait()
        for step in range(1, chips):
            for index in range(2):
                forward(index, head, step).wait()

        def one_block(step):
            target = chip_at(step)
            query = jnp.concatenate([qb[head, target], ones(rows)], axis=1)

            def piece(state, keys, masks, vals):
                keys = jnp.concatenate([keys, masks], axis=1)
                vals = jnp.concatenate([vals, ones(vals.shape[0])], axis=1)
                scores = lax.dot_general(
                    query, keys, (((1,), (1,)), ((), ())), preferred_element_type=jnp.float32
                )
                high = jnp.max(scores, axis=1, keepdims=True) * scale
                if state is not None:
                    high = jnp.maximum(high, state[0])
                weights = jnp.exp2(scores * scale - high).astype(jnp.bfloat16)
                mixed = jnp.dot(weights, vals, preferred_element_type=jnp.float32)
                if state is not None:
                    mixed = mixed + state[1] * jnp.exp2(state[0] - high)
                return (high, mixed)

            state = piece(None, tkb[head], tbias[...], tvb[head])
            for start in range(0, total, size):
                span = pl.ds(start, size)
                state = piece(state, kb[head, span], bias[span, :], vb[head, span])
            mixed = state[1]
            ob[head, target] = (
                mixed[:, :HEAD_DIM] / mixed[:, HEAD_DIM:HEAD_DIM + 1]
            ).astype(jnp.bfloat16)

        def far_block(step, _):
            one_block(step)
            out_copy(head, step).start()
            return 0

        lax.fori_loop(1, chips, far_block, 0)
        one_block(0)
        own_out(head).start()
        return 0

    lax.fori_loop(0, group, one_head, 0)

    def finish(head, _):
        for step in range(1, chips):
            out_copy(head, step).wait()
        own_out(head).wait()
        return 0

    lax.fori_loop(0, group, finish, 0)


def attention(queries, keys, values, text_keys, text_values, prompt_lengths, frame_counts, n):
    rows, width = queries.shape
    text = text_keys.shape[0]
    chips = n // CORES
    heads = width // HEAD_DIM
    group = heads // chips
    counts = jnp.broadcast_to(frame_counts.reshape(1, 1), (8, HEAD_DIM))
    lengths = jnp.broadcast_to(prompt_lengths.reshape(1, 1), (8, HEAD_DIM))
    bf16 = jnp.bfloat16
    total = n * rows
    hbm = pl.BlockSpec(memory_space=pl.ANY)
    vmem = pl.BlockSpec(memory_space=pltpu.VMEM)
    dma = pltpu.SemaphoreType.DMA
    return pl.pallas_call(
        functools.partial(attention_kernel, n, chips, group, rows, text),
        out_shape=jax.ShapeDtypeStruct((rows, width), bf16),
        in_specs=[hbm] * 5 + [vmem] * 2,
        out_specs=hbm,
        scratch_shapes=[
            pltpu.VMEM((group, chips, rows, HEAD_DIM), bf16),
            pltpu.VMEM((group, total, HEAD_DIM), bf16),
            pltpu.VMEM((group, total, HEAD_DIM), bf16),
            pltpu.VMEM((group, text, HEAD_DIM), bf16),
            pltpu.VMEM((group, text, HEAD_DIM), bf16),
            pltpu.VMEM((n, 8, HEAD_DIM), jnp.int32),
            pltpu.VMEM((total, HEAD_DIM), bf16),
            pltpu.VMEM((text, HEAD_DIM), bf16),
            pltpu.VMEM((group, chips, rows, HEAD_DIM), bf16),
            dma((3, group, chips - 1)),
            dma((3, group, chips - 1)),
            dma((2, group, chips)),
            dma((2, group, chips)),
            dma((n - 1,)),
            dma((n - 1,)),
            dma((3, group)),
            dma((2, group)),
            dma((group, chips)),
            dma((group, chips)),
        ],
        compiler_params=pltpu.CompilerParams(
            collective_id=0, has_side_effects=True, vmem_limit_bytes=62 * 1024 * 1024
        ),
    )(queries, keys, values, text_keys, text_values, counts, lengths)


def frame_valid(positions, counts_table, slots):
    frame_index = positions // slots
    slot_index = positions % slots
    frame_ids = jnp.arange(counts_table.shape[0], dtype=jnp.int32)
    frame_limit = jnp.sum(
        jnp.where(frame_index[:, None] == frame_ids[None, :], counts_table[None, :], 0), axis=1
    )
    return slot_index < frame_limit


def attend_block(carry, key_rows, value_rows, query_heads, key_mask):
    row_max, weight_sum, mixed_sum = carry
    head_count = query_heads.shape[1]
    key_heads = key_rows.reshape(key_rows.shape[0], head_count, HEAD_DIM)
    value_heads = value_rows.reshape(value_rows.shape[0], head_count, HEAD_DIM)
    scores = jnp.einsum(
        "qhd,khd->hqk", query_heads, key_heads, preferred_element_type=jnp.float32
    ) * HEAD_DIM ** (-0.5)
    scores = jnp.where(key_mask[None, None, :], scores, NEGATIVE)
    new_max = jnp.maximum(row_max, jnp.max(scores, axis=2))
    shrink = jnp.exp(row_max - new_max)
    weights = jnp.exp(scores - new_max[:, :, None])
    weight_sum = weight_sum * shrink + jnp.sum(weights, axis=2)
    mixed_sum = mixed_sum * shrink[:, :, None] + jnp.einsum(
        "hqk,khd->hqd",
        weights.astype(jnp.bfloat16),
        value_heads,
        preferred_element_type=jnp.float32,
    )
    return (new_max, weight_sum, mixed_sum)


def gathered_attention(
    queries, keys, values, text_keys, text_values, prompt_lengths, frame_counts, n
):
    row_count, head_cols = queries.shape
    head_count = head_cols // HEAD_DIM
    all_counts = lax.all_gather(frame_counts, "seq", axis=0, tiled=True)
    query_heads = queries.reshape(row_count, head_count, HEAD_DIM)
    text_mask = jnp.arange(text_keys.shape[0], dtype=jnp.int32) < prompt_lengths[0]
    empty_state = (
        jnp.full((head_count, row_count), NEGATIVE, jnp.float32),
        jnp.zeros((head_count, row_count), jnp.float32),
        jnp.zeros((head_count, row_count, HEAD_DIM), jnp.float32),
    )
    text_state = attend_block(empty_state, text_keys, text_values, query_heads, text_mask)
    key_rows = lax.all_gather(keys, "seq", axis=0, tiled=True)
    value_rows = lax.all_gather(values, "seq", axis=0, tiled=True)
    positions = jnp.arange(key_rows.shape[0], dtype=jnp.int32)
    _, weight_sum, mixed_sum = attend_block(
        text_state, key_rows, value_rows, query_heads,
        frame_valid(positions, all_counts, row_count // frame_counts.shape[0]),
    )
    return (
        jnp.transpose(mixed_sum / weight_sum[:, :, None], (1, 0, 2))
        .reshape(row_count, head_cols)
        .astype(jnp.bfloat16)
    )


def body(n, cfgs, queries, keys, values, text_keys, text_values, prompt_lengths, frame_counts, out_weight):
    rows, head_cols = queries.shape[1:]
    split = n % CORES == 0 and (head_cols // HEAD_DIM) % (n // CORES) == 0
    attend = attention if split and frame_counts.shape[0] == 1 else gathered_attention
    attended = attend(
        queries[0], keys[0], values[0], text_keys[0], text_values[0],
        prompt_lengths, frame_counts, n,
    )
    branch = lax.psum_scatter(
        lax.dot_general(
            out_weight, attended, (((0,), (1,)), ((), ())), preferred_element_type=jnp.float32
        ).astype(jnp.bfloat16),
        "tp",
        scatter_dimension=0,
        tiled=True,
    )
    half = branch.shape[0] // cfgs
    mine = lax.axis_index("cfg")
    kept = lax.dynamic_slice_in_dim(branch, mine * half, half, 0)
    given = lax.dynamic_slice_in_dim(branch, (1 - mine) * half, half, 0)
    other = lax.ppermute(given, "cfg", [(0, 1), (1, 0)])
    first = mine == 0
    conditional = jnp.where(first, kept, other).astype(jnp.float32)
    unconditional = jnp.where(first, other, kept).astype(jnp.float32)
    guided = unconditional + GUIDANCE * (conditional - unconditional)
    valid = (jnp.arange(rows, dtype=jnp.int32) < frame_counts[0])[None, :]

    def local_sum(field):
        return jnp.sum(jnp.where(valid, field, 0.0), axis=1)

    sums = lax.psum(
        jnp.stack([
            local_sum(guided),
            local_sum(guided * guided),
            local_sum(conditional),
            local_sum(conditional * conditional),
            jnp.full((half,), frame_counts[0].astype(jnp.float32)),
        ]),
        "seq",
    )
    means = sums[:4] / sums[4:5]
    guided_mean = means[0]
    guided_var = means[1] - guided_mean * guided_mean
    cond_var = means[3] - means[2] * means[2]
    std_ratio = jnp.sqrt((cond_var + 1.0) / (guided_var + 1.0))
    factor = RESCALE * std_ratio + (1.0 - RESCALE)
    velocity = guided_mean[:, None] + (guided - guided_mean[:, None]) * factor[:, None]
    return velocity.astype(jnp.bfloat16).T


def solution(mesh):
    placed = (
        P("cfg", "seq", "tp"),
        P("cfg", "seq", "tp"),
        P("cfg", "seq", "tp"),
        P("cfg", None, "tp"),
        P("cfg", None, "tp"),
        P("cfg"),
        P("seq"),
        P("tp", None),
    )
    return jax.shard_map(
        functools.partial(body, mesh.shape["seq"], mesh.shape["cfg"]),
        mesh=mesh, in_specs=placed, out_specs=P("seq", ("tp", "cfg")), check_vma=False,
    )
```

time: 639 us -> 383 us (0.60)
  Pallas kernels: 0 us -> 218 us
  waiting for transfers between devices: 292 us -> 92.4 us
  matrix products: 165 us -> 20 us
  local copies, waits for them, and re-layouts: 65.8 us -> 2.66 us
  other arithmetic: 59.5 us -> 4.89 us
  blocking collectives: 39 us -> 27.9 us
    all_gather x3 -> x0, waiting for transfers between devices: 231 us -> none  [the longest x1 141 us: body(): key_rows = lax.all_gather(keys[0], 'seq', axis=0, tiled=True)]
    pallas_call x0 -> x1, Pallas kernels: none -> 218 us  [attention(): pl.pallas_call(functools.partial(attention_kernel, n, chips, group, rows,...]
    dot_general x8 -> x0, matrix products: 145 us -> none  [the longest x2 70.7 us: attend_block(): jnp.einsum('qhd,khd->hqk', query_heads, key_heads, preferred_element_type...]
    reduce_sum x4 -> x1, other arithmetic: 56 us -> 3.09 us  [local_sum(): return jnp.sum(jnp.where(valid, field, 0.0), axis=1)]
    all_gather x2 -> x0, local copies, waits for them, and re-layouts: 49.5 us -> none  [the longest x1 25.5 us: body(): key_rows = lax.all_gather(keys[0], 'seq', axis=0, tiled=True)]
    ppermute x0 -> x1, waiting for transfers between devices: none -> 27.2 us  [body(): other = lax.ppermute(given, 'cfg', [(0, 1), (1, 0)])]
    unnamed x16 -> x0, local copies, waits for them, and re-layouts: 13.4 us -> none
    unnamed x1 -> x0, blocking collectives: 10.6 us -> none
  transfers between devices with their start and end apart: 4 -> 2, of which waited for: 4 -> 2; matrix products, arithmetic and copies ran while one was open for 28% -> 0% of each run, Pallas kernels for 0% -> 0%
where the time goes in v1:
time: 383 us
  Pallas kernels  218 us (57%)
  waiting for transfers between devices  92.4 us (24%)
  blocking collectives  27.9 us (7%)
  matrix products  20 us (5%)
  between operations  14.8 us (4%)
  other arithmetic  4.89 us (1%)
    pallas_call x1, Pallas kernels, attention(): pl.pallas_call(functools.partial(attention_kernel, n, chips, group, rows,...  218 us
    reduce_scatter x1, waiting for transfers between devices, body(): lax.psum_scatter(lax.dot_general(out_weight, attended, (((0,), (1,)), (()...  65.1 us
    psum x1, blocking collectives, body(): lax.psum(jnp.stack([local_sum(guided), local_sum(guided * guided), local_...  27.9 us
    ppermute x1, waiting for transfers between devices, body(): other = lax.ppermute(given, 'cfg', [(0, 1), (1, 0)])  27.2 us
    dot_general x1, matrix products, body(): lax.dot_general(out_weight, attended, (((0,), (1,)), ((), ())), preferred...  20 us
  transfers between devices with their start and end apart: 2, of which 2 were waited for; matrix products, arithmetic and copies ran while one was open for 0% of the time, Pallas kernels for 0%

profile of v1, /device:TPU:0, one launch (start us, length us, event | category | flops | bytes accessed | tf_op | source)
XLA Modules:
  0.0 382.5 jit_solution(9761364226135961163)
XLA Ops:
  6.5 0.0 reduce-scatter.2.cloned.1.call-start
  7.8 0.6 broadcast_in_dim.39.counts
  8.4 0.6 broadcast_in_dim.41.lengths
  9.0 218.4 %shard_map.82 = bf16[480,2560]{1,0:T(8,128)(2,1)} custom-call(bf16[480,2560]{1,0:T(8,128)(2,1)} %bitcast.19, bf16[480,2560]{1,0:T(8,128)(2,1)} %bitcast.20, bf16[480,2560]{1,0:T(8,128)(2,1)} %bitcast.21, bf16[512,2560]{1,0:T(8,128)(2,1)} %bitcast.17, bf16[512,2560]{1,0:T(8,128)(2,1)} %bitcast.18, s32[8,128]{1,0:T(8,128)} %broadcast_in_dim.39.counts, ...), custom_call_target="tpu_custom_call" | custom-call | tf_op jit(solution)/shard_map/pallas_call | solution.py:238
  227.5 20.0 %fusion = bf16[5120,480]{0,1:T(8,128)(2,1)} fusion(bf16[480,2560]{1,0:T(8,128)(2,1)} %shard_map.82, bf16[2560,5120]{1,0:T(8,128)(2,1)} %param.15), kind=kOutput, calls=%fused_computation.1 | convolution fusion | flops 12585369600 | bytes 33587200 | tf_op jit(solution)/shard_map/dot_general | solution.py:339
  247.4 0.0 reduce-scatter.2.cloned.1.call-update
  247.5 65.1 %reduce-scatter.2.cloned.1.call-done = bf16[2560,480]{0,1:T(8,128)(2,1)} async-done(((bf16[5120,480]{0,1:T(8,128)(2,1)}), bf16[2560,480]{0,1:T(8,128)(2,1)}) %reduce-scatter.2.cloned.1.call-update) | async-done | bytes 2457616 | tf_op jit(solution)/shard_map/reduce_scatter | solution.py:338
  312.6 1.4 constant_dynamic-slice_fusion
  314.0 1.5 collective-permute-start
  315.5 27.2 %collective-permute-done = bf16[1280,480]{0,1:T(8,128)(2,1)} collective-permute-done((bf16[1280,480]{0,1:T(8,128)(2,1)S(1)}, bf16[1280,480]{0,1:T(8,128)(2,1)}, u32[]{:S(2)}, u32[]{:S(2)}) %collective-permute-start) | collective-permute-done | bytes 1228832 | tf_op jit(solution)/shard_map/ppermute | solution.py:350
  342.8 3.1 select_reduce_fusion
  345.9 0.1 stack.19
  346.0 27.9 %psum.7 = f32[5,1280]{1,0:T(8,128)S(1)} all-reduce(f32[5,1280]{1,0:T(8,128)S(1)} %stack.19), channel_id=1, replica_groups=mesh['cfg'=2,'seq'=8,'tp'=2] {'seq'}, use_global_device_ids=true, to_apply=%region_5.6 | all-reduce | flops 6400 | bytes 51200 | tf_op jit(solution)/shard_map/psum | solution.py:360
  374.0 1.7 fusion.5
  (10 shorter events, 0.1 us)
Async XLA Ops:
  6.5 306.1 %reduce-scatter.2.cloned.1.call-start = ((), (), s32[]{:S(2)}) async-start(), calls=%async_computation.1 | async-start | bytes 7372800 | tf_op jit(solution)/shard_map/reduce_scatter | solution.py:338
  314.0 28.8 %collective-permute-start = (bf16[1280,480]{0,1:T(8,128)(2,1)S(1)}, bf16[1280,480]{0,1:T(8,128)(2,1)}, u32[]{:S(2)}, u32[]{:S(2)}) collective-permute-start(bf16[1280,480]{0,1:T(8,128)(2,1)S(1)} %constant_dynamic-slice_fusion), channel_id=1, source_target_pairs={{0,16},{16,0},{1,17},{17,1},{2,18},{18,2},{3,19},{19,3},{4,20},{20... | collective-permute-start | bytes 3686408 | tf_op jit(solution)/shard_map/ppermute | solution.py:350
Sparse Core Ops, SparseCore 0:
  247.6 64.9 reduce-scatter.1

commit v2 on v1

--- a/solution.py
+++ b/solution.py
@@ -327,7 +327,180 @@
     )
 
 
-def body(n, cfgs, queries, keys, values, text_keys, text_values, prompt_lengths, frame_counts, out_weight):
+PIECES = 2
+
+
+def tail_kernel(
+    n, rows, part,
+    att, w, counts,
+    out,
+    ab, wb, sb, rb, own, yb, yr, gb, st, sg,
+    asem, wsem, xsend, xrecv, ysend, yrecv, ssend, srecv,
+):
+    me = lax.axis_index("seq")
+    t = lax.axis_index("tp")
+    c = lax.axis_index("cfg")
+    steps = 2 * PIECES
+    width = PIECES * part
+
+    def column(side, index):
+        far = lax.div(index, PIECES)
+        branch = far * c + (1 - far) * (1 - c)
+        return (side * 2 + branch) * width + lax.rem(index, PIECES) * part
+
+    def weight_copy(j):
+        far = lax.div(j, steps)
+        side = far * t + (1 - far) * (1 - t)
+        start = pl.multiple_of(column(side, lax.rem(j, steps)), HEAD_DIM)
+        return pltpu.make_async_copy(w.at[:, pl.ds(start, part)], wb.at[j], wsem.at[j])
+
+    load = pltpu.make_async_copy(att, ab, asem)
+    load.start()
+
+    def start_weight(j, _):
+        weight_copy(j).start()
+        return 0
+
+    lax.fori_loop(0, 2 * steps, start_weight, 0)
+
+    barrier = pltpu.get_barrier_semaphore()
+    pl.semaphore_signal(barrier, inc=1, device_id={"tp": 1 - t}, device_id_type=MESH)
+    pl.semaphore_signal(barrier, inc=1, device_id={"cfg": 1 - c}, device_id_type=MESH)
+    for step in range(1, n):
+        pl.semaphore_signal(
+            barrier, inc=1, device_id={"seq": lax.rem(me + step, n)}, device_id_type=MESH
+        )
+    pl.semaphore_wait(barrier, n + 1)
+
+    def x_copy(i):
+        return pltpu.make_async_remote_copy(
+            src_ref=sb.at[i], dst_ref=rb.at[i], send_sem=xsend.at[i], recv_sem=xrecv.at[i],
+            device_id={"tp": 1 - t}, device_id_type=MESH,
+        )
+
+    def y_copy(i):
+        return pltpu.make_async_remote_copy(
+            src_ref=yb.at[i], dst_ref=yr.at[i], send_sem=ysend.at[i], recv_sem=yrecv.at[i],
+            device_id={"cfg": 1 - c}, device_id_type=MESH,
+        )
+
+    def stat_copy(step):
+        return pltpu.make_async_remote_copy(
+            src_ref=st, dst_ref=sg.at[me], send_sem=ssend.at[step - 1],
+            recv_sem=srecv.at[step - 1],
+            device_id={"seq": lax.rem(me + step, n)}, device_id_type=MESH,
+        )
+
+    load.wait()
+
+    def project(j):
+        weight_copy(j).wait()
+        return jnp.dot(ab[...], wb[j], preferred_element_type=jnp.float32)
+
+    def given(i, _):
+        sb[i] = project(i).astype(jnp.bfloat16)
+        x_copy(i).start()
+        return 0
+
+    def kept(i, _):
+        own[i] = project(steps + i)
+        return 0
+
+    lax.fori_loop(0, steps, given, 0)
+    lax.fori_loop(0, steps, kept, 0)
+
+    def across(i, _):
+        x_copy(i).wait()
+        yb[i] = (own[i] + rb[i].astype(jnp.float32)).astype(jnp.bfloat16)
+        y_copy(i).start()
+        return 0
+
+    lax.fori_loop(0, PIECES, across, 0)
+
+    limit = counts[0:1, 0:1]
+    valid = lax.broadcasted_iota(jnp.int32, (rows, part), 0) < limit
+    first = jnp.full((rows, part), c, jnp.int32) == 0
+    st[...] = jnp.zeros_like(st)
+    for i in range(PIECES):
+        span = pl.ds(i * part, part)
+        x_copy(PIECES + i).wait()
+        mine = (own[PIECES + i] + rb[PIECES + i].astype(jnp.float32)).astype(jnp.bfloat16)
+        mine = mine.astype(jnp.float32)
+        y_copy(i).wait()
+        other = yr[i].astype(jnp.float32)
+        conditional = jnp.where(first, mine, other)
+        unconditional = jnp.where(first, other, mine)
+        guided = unconditional + GUIDANCE * (conditional - unconditional)
+        gb[:, span] = guided
+        guided = jnp.where(valid, guided, 0.0)
+        conditional = jnp.where(valid, conditional, 0.0)
+        for row, field in enumerate(
+            (guided, guided * guided, conditional, conditional * conditional)
+        ):
+            st[row:row + 1, span] = jnp.sum(field, axis=0, keepdims=True)
+        st[4:5, span] = jnp.broadcast_to(limit.astype(jnp.float32), (1, part))
+
+    for step in range(1, n):
+        stat_copy(step).start()
+    sg[me] = st[...]
+    for step in range(1, n):
+        stat_copy(step).wait()
+    sums = sg[0]
+    for source in range(1, n):
+        sums = sums + sg[source]
+    valid_total = sums[4:5, :]
+    guided_mean = sums[0:1, :] / valid_total
+    guided_var = sums[1:2, :] / valid_total - guided_mean * guided_mean
+    cond_mean = sums[2:3, :] / valid_total
+    cond_var = sums[3:4, :] / valid_total - cond_mean * cond_mean
+    std_ratio = jnp.sqrt((cond_var + 1.0) / (guided_var + 1.0))
+    factor = RESCALE * std_ratio + (1.0 - RESCALE)
+    out[...] = (guided_mean + (gb[...] - guided_mean) * factor).astype(jnp.bfloat16)
+
+
+def fused_tail(attended, out_weight, frame_counts, n):
+    rows, depth = attended.shape
+    width = out_weight.shape[1] // 4
+    part = width // PIECES
+    steps = 2 * PIECES
+    bf16 = jnp.bfloat16
+    f32 = jnp.float32
+    counts = jnp.broadcast_to(frame_counts.reshape(1, 1), (8, HEAD_DIM))
+    hbm = pl.BlockSpec(memory_space=pl.ANY)
+    vmem = pl.BlockSpec(memory_space=pltpu.VMEM)
+    dma = pltpu.SemaphoreType.DMA
+    return pl.pallas_call(
+        functools.partial(tail_kernel, n, rows, part),
+        out_shape=jax.ShapeDtypeStruct((rows, width), bf16),
+        in_specs=[hbm, hbm, vmem],
+        out_specs=vmem,
+        scratch_shapes=[
+            pltpu.VMEM((rows, depth), bf16),
+            pltpu.VMEM((2 * steps, depth, part), bf16),
+            pltpu.VMEM((steps, rows, part), bf16),
+            pltpu.VMEM((steps, rows, part), bf16),
+            pltpu.VMEM((steps, rows, part), f32),
+            pltpu.VMEM((PIECES, rows, part), bf16),
+            pltpu.VMEM((PIECES, rows, part), bf16),
+            pltpu.VMEM((rows, width), f32),
+            pltpu.VMEM((8, width), f32),
+            pltpu.VMEM((n, 8, width), f32),
+            dma,
+            dma((2 * steps,)),
+            dma((steps,)),
+            dma((steps,)),
+            dma((PIECES,)),
+            dma((PIECES,)),
+            dma((n - 1,)),
+            dma((n - 1,)),
+        ],
+        compiler_params=pltpu.CompilerParams(
+            collective_id=1, has_side_effects=True, vmem_limit_bytes=62 * 1024 * 1024
+        ),
+    )(attended, out_weight, counts)
+
+
+def body(n, cfgs, tps, queries, keys, values, text_keys, text_values, prompt_lengths, frame_counts, out_weight):
     rows, head_cols = queries.shape[1:]
     split = n % CORES == 0 and (head_cols // HEAD_DIM) % (n // CORES) == 0
     attend = attention if split and frame_counts.shape[0] == 1 else gathered_attention
@@ -335,6 +508,9 @@
         queries[0], keys[0], values[0], text_keys[0], text_values[0],
         prompt_lengths, frame_counts, n,
     )
+    whole = out_weight.shape[1] % (4 * PIECES * HEAD_DIM) == 0
+    if cfgs == 2 and tps == 2 and whole and frame_counts.shape[0] == 1:
+        return fused_tail(attended, out_weight, frame_counts, n)
     branch = lax.psum_scatter(
         lax.dot_general(
             out_weight, attended, (((0,), (1,)), ((), ())), preferred_element_type=jnp.float32
@@ -389,6 +565,6 @@
         P("tp", None),
     )
     return jax.shard_map(
-        functools.partial(body, mesh.shape["seq"], mesh.shape["cfg"]),
+        functools.partial(body, mesh.shape["seq"], mesh.shape["cfg"], mesh.shape["tp"]),
         mesh=mesh, in_specs=placed, out_specs=P("seq", ("tp", "cfg")), check_vma=False,
     )

time: 383 us -> 296 us (0.77)
  waiting for transfers between devices: 92.4 us -> 0 us
  Pallas kernels: 218 us -> 291 us
  blocking collectives: 27.9 us -> 0 us
  matrix products: 20 us -> 0 us
  between operations: 14.8 us -> 1.31 us
  other arithmetic: 4.89 us -> 0 us
    pallas_call x0 -> x1, Pallas kernels: none -> 72.5 us  [fused_tail(): pl.pallas_call(functools.partial(tail_kernel, n, rows, part), out_shape=j...]
    reduce_scatter x1 -> x0, waiting for transfers between devices: 65.1 us -> none  [body(): lax.psum_scatter(lax.dot_general(out_weight, attended, (((0,), (1,)), (()...]
    psum x1 -> x0, blocking collectives: 27.9 us -> none  [body(): lax.psum(jnp.stack([local_sum(guided), local_sum(guided * guided), local_...]
    ppermute x1 -> x0, waiting for transfers between devices: 27.2 us -> none  [body(): other = lax.ppermute(given, 'cfg', [(0, 1), (1, 0)])]
    dot_general x1 -> x0, matrix products: 20 us -> none  [body(): lax.dot_general(out_weight, attended, (((0,), (1,)), ((), ())), preferred...]
  transfers between devices with their start and end apart: 2 -> 0, of which waited for: 2 -> 0; matrix products, arithmetic and copies ran while one was open for 0% -> 0% of each run, Pallas kernels for 0% -> 0%
where the time goes in v2:
time: 296 us
  Pallas kernels  291 us (98%)
  local copies, waits for them, and re-layouts  3.58 us (1%)
    pallas_call x1, Pallas kernels, attention(): pl.pallas_call(functools.partial(attention_kernel, n, chips, group, rows,...  218 us
    pallas_call x1, Pallas kernels, fused_tail(): pl.pallas_call(functools.partial(tail_kernel, n, rows, part), out_shape=j...  72.5 us

profile of v2, /device:TPU:0, one launch (start us, length us, event | category | flops | bytes accessed | tf_op | source)
XLA Modules:
  0.0 295.8 jit_solution(1270971306080289301)
XLA Ops:
  1.3 0.6 broadcast_in_dim.18.counts
  1.9 0.6 broadcast_in_dim.20.lengths
  2.5 218.4 %shard_map.82.att = bf16[480,2560]{1,0:T(8,128)(2,1)} custom-call(bf16[480,2560]{1,0:T(8,128)(2,1)} %bitcast.11, bf16[480,2560]{1,0:T(8,128)(2,1)} %bitcast.12, bf16[480,2560]{1,0:T(8,128)(2,1)} %bitcast.13, bf16[512,2560]{1,0:T(8,128)(2,1)} %bitcast.9, bf16[512,2560]{1,0:T(8,128)(2,1)} %bitcast.10, s32[8,128]{1,0:T(8,128)} %broadcast_in_dim.18.counts, ...), custom_call_target="tpu_custom_call" | custom-call | tf_op jit(solution)/shard_map/pallas_call | solution.py:238
  220.9 72.5 %shard_map.83 = bf16[480,1280]{1,0:T(8,128)(2,1)} custom-call(bf16[480,2560]{1,0:T(8,128)(2,1)} %shard_map.82.att, bf16[2560,5120]{1,0:T(8,128)(2,1)} %w.1, s32[8,128]{1,0:T(8,128)} %broadcast_in_dim.18.counts), custom_call_target="tpu_custom_call" | custom-call | tf_op jit(solution)/shard_map/pallas_call | solution.py:472
  293.4 2.4 copy.12

commit v3 on v2

--- a/solution.py
+++ b/solution.py
@@ -327,7 +327,7 @@
     )
 
 
-PIECES = 2
+PIECES = 5
 
 
 def tail_kernel(

time: 296 us -> 294 us (level)
  no operation moved by 1% of the time
where the time goes in v3:
time: 294 us; the launch traced here: 293 us
  Pallas kernels  289 us (98%)
  local copies, waits for them, and re-layouts  3.58 us (1%)
    pallas_call x1, Pallas kernels, attention(): pl.pallas_call(functools.partial(attention_kernel, n, chips, group, rows,...  218 us
    pallas_call x1, Pallas kernels, fused_tail(): pl.pallas_call(functools.partial(tail_kernel, n, rows, part), out_shape=j...  70.2 us

profile of v3, /device:TPU:0, one launch (start us, length us, event | category | flops | bytes accessed | tf_op | source)
XLA Modules:
  0.0 293.5 jit_solution(13215650715575794454)
XLA Ops:
  1.3 0.6 broadcast_in_dim.18.counts
  1.9 0.6 broadcast_in_dim.20.lengths
  2.5 218.4 %shard_map.82.att = bf16[480,2560]{1,0:T(8,128)(2,1)} custom-call(bf16[480,2560]{1,0:T(8,128)(2,1)} %bitcast.11, bf16[480,2560]{1,0:T(8,128)(2,1)} %bitcast.12, bf16[480,2560]{1,0:T(8,128)(2,1)} %bitcast.13, bf16[512,2560]{1,0:T(8,128)(2,1)} %bitcast.9, bf16[512,2560]{1,0:T(8,128)(2,1)} %bitcast.10, s32[8,128]{1,0:T(8,128)} %broadcast_in_dim.18.counts, ...), custom_call_target="tpu_custom_call" | custom-call | tf_op jit(solution)/shard_map/pallas_call | solution.py:238
  220.9 70.2 %shard_map.83 = bf16[480,1280]{1,0:T(8,128)(2,1)} custom-call(bf16[480,2560]{1,0:T(8,128)(2,1)} %shard_map.82.att, bf16[2560,5120]{1,0:T(8,128)(2,1)} %w.1, s32[8,128]{1,0:T(8,128)} %broadcast_in_dim.18.counts), custom_call_target="tpu_custom_call" | custom-call | tf_op jit(solution)/shard_map/pallas_call | solution.py:472
  291.1 2.4 copy.12
